TPU v7x, 512 devices: a whole 4x8x8 slice. The times are simulated.
512 devices in a mesh: slab: 64 (over z, y_hi, core), load: 8 (over x, y_lo).
Axes of the slice: x: 4, y: 8 (y_hi: 4, y_lo: 2; y = y_hi * 2 + y_lo), z: 8, core: 2. Of those that a mesh axis runs over, the one named last changes fastest.
Arguments:
- density: float32 [256, 16, 128], P('slab'), may hold values from 0.05 to 1
- passive: int32 [256, 16, 128], P('slab'), may hold values 0 or 1
- fixed: int32 [256, 16, 128], P('slab'), may hold values 0 or 1
- u_start: float32 [8, 3, 256, 16, 128], P('load', None, 'slab'), may hold values from -4 to 4
- load_nodes: int32 [8, 64], P('load'), may hold values from 0 to 524287
- load_forces: float32 [8, 3, 64], P('load'), may hold values from -6 to 6
Outputs:
- new_density: float32 [256, 16, 128], P('slab', 'load')
- displacement: float32 [8, 3, 256, 16, 128], P('load', None, 'slab')
All inputs are finite; a program needn't handle non-finite values. No bound on the sum of `passive` or of `fixed` on one device may be relied on, other than what follows from the above.
Results may differ from a plain program's by a relative error of at most 0.0003.
Values sent between devices are 32-bit elements; how exact they have to be, the bound alone decides.
A program may use at most 64 MiB of HBM per device.

v0:
```python
import functools
import math

import jax
import jax.numpy as jnp
import numpy as np
from jax import lax
from jax.sharding import Mesh
from jax.sharding import PartitionSpec as P

SWEEPS = 3
UPDATES = 2
SLAB = ("slab_0", "slab_1", "slab_2")


young_floor = 0.001
density_floor = 0.001
move_limit = 0.2
sens_shift = 0.001


def with_halo(cells, sides, width):
    for axis, dim in sides:
        count = lax.axis_size(axis)
        ends = count - 1
        head = lax.slice_in_dim(cells, 0, width, axis=dim)
        tail = lax.slice_in_dim(cells, cells.shape[dim] - width, cells.shape[dim], axis=dim)
        cells = jnp.concatenate(
            [
                lax.ppermute(tail, axis, [(i, (i + 1) % count) for i in range(ends)]),
                cells,
                lax.ppermute(head, axis, [((i + 1) % count, i) for i in range(ends)]),
            ],
            axis=dim,
        )
    return cells


def passed_along(value, axis, steps):
    count = lax.axis_size(axis)
    leading, last = (max(0, -steps), min(count, count - steps))
    return lax.ppermute(value, axis, [(source, source + steps) for source in range(leading, last)])


def from_everyone(shard, axis):
    copies = jnp.broadcast_to(shard, (lax.axis_size(axis), *shard.shape))
    return lax.all_to_all(copies, axis, split_axis=0, concat_axis=0, tiled=True)


def over_copies(shard, axis):
    everything = from_everyone(shard, axis)
    return jnp.sum(everything, axis=0)


def by_axis(shard, axes):
    return functools.reduce(lax.psum, axes, shard)


def diagonal_of(matrix):
    return np.array([matrix[entry, entry] for entry in range(matrix.shape[0])])


def element_stiffness():
    poisson = 0.3
    lame_first = poisson / ((1.0 + poisson) * (1.0 - 2.0 * poisson))
    lame_second = 1.0 / (2.0 * (1.0 + poisson))
    elastic = np.zeros((6, 6))
    elastic[:3, :3] = lame_first
    for axis_pos in range(3):
        elastic[axis_pos, axis_pos] += 2.0 * lame_second
        elastic[axis_pos + 3, axis_pos + 3] = lame_second
    points = [0.5 - 0.5 / math.sqrt(3.0), 0.5 + 0.5 / math.sqrt(3.0)]
    matrix = np.zeros((24, 24))
    for point_x in points:
        for point_y in points:
            for point_z in points:
                strain = np.zeros((6, 24))
                for corner in range(8):
                    shift_x = corner % 2
                    shift_y = corner // 2 % 2
                    shift_z = corner // 4
                    value_x = point_x if shift_x else 1.0 - point_x
                    value_y = point_y if shift_y else 1.0 - point_y
                    value_z = point_z if shift_z else 1.0 - point_z
                    slope_x = 1.0 if shift_x else -1.0
                    slope_y = 1.0 if shift_y else -1.0
                    slope_z = 1.0 if shift_z else -1.0
                    grad_x = slope_x * value_y * value_z
                    grad_y = value_x * slope_y * value_z
                    grad_z = value_x * value_y * slope_z
                    column = 3 * corner
                    strain[0, column] = grad_x
                    strain[1, column + 1] = grad_y
                    strain[2, column + 2] = grad_z
                    strain[3, column] = grad_y
                    strain[3, column + 1] = grad_x
                    strain[4, column + 1] = grad_z
                    strain[4, column + 2] = grad_y
                    strain[5, column] = grad_z
                    strain[5, column + 2] = grad_x
                matrix += strain.T @ elastic @ strain / 8.0
    return matrix


def spectrum_top(matrix):
    diag_np = diagonal_of(matrix)
    scaled = matrix / np.sqrt(np.outer(diag_np, diag_np))
    vector = np.linspace(1.0, 2.0, 24)
    for repeat in range(500):
        vector = scaled @ vector
        vector = vector / np.sqrt(np.sum(vector * vector))
    return float(vector @ scaled @ vector)


def cheb_constants(matrix):
    upper_bound = 1.05 * spectrum_top(matrix)
    lower_bound = upper_bound / 12.0
    center = 0.5 * (upper_bound + lower_bound)
    half_width = 0.5 * (upper_bound - lower_bound)
    return (center, half_width, center / half_width)


def cheb_weights(count, half_width, ratio_sigma):
    weights = []
    current = 1.0 / ratio_sigma
    for iteration in range(count):
        following = 1.0 / (2.0 * ratio_sigma - current)
        weights.append((following * current, 2.0 * following / half_width))
        current = following
    return weights


def element_values(field):
    planes = field.shape[2] - 1
    rows = field.shape[3]
    cols = field.shape[4]
    padded = jnp.pad(field, ((0, 0), (0, 0), (0, 0), (0, 1), (0, 1)))
    pieces = []
    for corner in range(8):
        shift_x = corner % 2
        shift_y = corner // 2 % 2
        shift_z = corner // 4
        pieces.append(
            padded[
                :, :, shift_z : shift_z + planes, shift_y : shift_y + rows, shift_x : shift_x + cols
            ]
        )
    stacked = jnp.stack(pieces, axis=1)
    return stacked.reshape(field.shape[0], 24, planes, rows, cols)


def spread_nodes(forces):
    cases, planes, rows, cols = (forces.shape[0], forces.shape[2], forces.shape[3], forces.shape[4])
    split = forces.reshape(cases, 8, 3, planes, rows, cols)
    total = jnp.zeros((cases, 3, planes + 1, rows + 1, cols + 1), jnp.float32)
    for corner in range(8):
        shift_x = corner % 2
        shift_y = corner // 2 % 2
        shift_z = corner // 4
        total = total + jnp.pad(
            split[:, corner],
            (
                (0, 0),
                (0, 0),
                (shift_z, 1 - shift_z),
                (shift_y, 1 - shift_y),
                (shift_x, 1 - shift_x),
            ),
        )
    return total[:, :, :, :rows, :cols]


def stiff_apply(values, table):
    return jnp.einsum("ij,cjzyx->cizyx", table, values, precision=lax.Precision.HIGHEST)


def with_margin(field):
    return with_halo(field, ((SLAB, 2),), 1)


def nodes_local(terms):
    planes = terms.shape[2] - 1
    return spread_nodes(terms)[:, :, 1 : planes + 1]


def body(density, passive, fixed, u_start, load_nodes, load_forces):
    stiff_numpy = element_stiffness()
    center, half_width, ratio_sigma = cheb_constants(stiff_numpy)
    table = jnp.asarray(stiff_numpy, jnp.float32)
    planes, rows, cols = density.shape
    count = planes * rows * cols
    free = (1 - fixed).astype(jnp.float32)
    void = passive == 1
    active = (1 - passive).astype(jnp.float32)
    design = jnp.where(void, jnp.float32(density_floor), density)
    offset = lax.axis_index(SLAB) * count

    def place(nodes, values):
        local = nodes - offset
        inside = (local >= 0) & (local < count)
        local = jnp.where(inside, local, count)
        return jnp.zeros((3, count), jnp.float32).at[:, local].add(values, mode="drop")

    loads = jax.vmap(place)(load_nodes, load_forces).reshape(
        load_nodes.shape[0], 3, planes, rows, cols
    )
    diag_table = jnp.asarray(diagonal_of(stiff_numpy), jnp.float32)
    weights = cheb_weights(SWEEPS, half_width, ratio_sigma)
    share = rows // lax.axis_size("load")
    first_row = lax.axis_index("load") * share
    displace = u_start
    result_density = design
    for update in range(UPDATES):
        young = young_floor + (1.0 - young_floor) * design * design * design
        below = passed_along(young[planes - 1 :], SLAB, 1)
        young_wide = jnp.concatenate([below, young], axis=0)
        diagonal = nodes_local(young_wide[None, None] * diag_table[None, :, None, None, None])

        def operate(field):
            values = element_values(with_margin(field))
            return nodes_local(young_wide[None, None] * stiff_apply(values, table))

        inverse = free / diagonal
        displace = displace * free
        residual = free * (loads - operate(displace))
        direction = inverse * residual / center
        for iteration in range(SWEEPS):
            displace = displace + direction
            if iteration < SWEEPS - 1:
                residual = residual - free * operate(direction)
                keep, push = weights[iteration]
                direction = keep * direction + push * inverse * residual
        values = element_values(with_margin(displace)[:, :, 1:])
        energy = jnp.sum(jnp.sum(values * stiff_apply(values, table), axis=1), axis=0)
        total = over_copies(energy, "load")
        quantity = design * jnp.sqrt(
            3.0 * design * design * (1.0 - young_floor) * total + sens_shift
        )
        sums = (by_axis(jnp.sum(quantity * active), SLAB), by_axis(jnp.sum(design * active), SLAB))
        scale = sums[0] / sums[1]
        lower = jnp.maximum(density_floor, design - move_limit)
        upper = jnp.minimum(1.0, design + move_limit)
        design = jnp.where(
            void, jnp.float32(density_floor), jnp.clip(quantity / scale, lower, upper)
        )
        result_density = lax.dynamic_slice_in_dim(design, first_row, share, 1)
    return (result_density, displace)


def solution(mesh):
    finer = Mesh(
        mesh.devices.reshape(8, 4, 2, mesh.shape["load"]), ("slab_0", "slab_1", "slab_2", "load")
    )
    placed = (
        P(SLAB, None, None),
        P(SLAB, None, None),
        P(SLAB, None, None),
        P("load", None, SLAB, None, None),
        P("load", None),
        P("load", None, None),
    )
    return jax.shard_map(
        body,
        mesh=finer,
        in_specs=placed,
        out_specs=(P(SLAB, "load", None), P("load", None, SLAB, None, None)),
        check_vma=False,
    )
```

profile of v0, /device:TPU:1, one launch (start us, length us, event | category | flops | bytes accessed | tf_op | source)
XLA Modules:
  0.0 210.0 jit_solution(13408490376994404235)
XLA Ops:
  1.4 5.6 %collective-permute-start = (f32[1,16,128]{2,1,0:T(8,128)S(1)}, f32[1,16,128]{2,1,0:T(8,128)S(1)}, u32[]{:S(2)}, u32[]{:S(2)}) collective-permute-start(f32[1,16,128]{2,1,0:T(8,128)S(1)} %slice.616), channel_id=1, source_target_pairs={{0,8},{8,16},{16,24},{24,32},{32,40},{40,48},{48,56},{56,64},{64,7... | collective-permute-start | bytes 24584 | tf_op jit(solution)/shard_map/ppermute | solution.py:42
  8.7 1.9 collective-permute-start.1
  10.7 3.8 %collective-permute-start.2 = (f32[1,3,1,16,128]{4,3,2,1,0:T(8,128)S(1)}, f32[1,3,1,16,128]{4,3,2,1,0:T(8,128)S(1)}, u32[]{:S(2)}, u32[]{:S(2)}) collective-permute-start(f32[1,3,1,16,128]{4,3,2,1,0:T(8,128)S(1)} %get-tuple-element.97), channel_id=1, source_target_pairs={{8,0},{16,8},{24,16},{32,24},{40,32},{48,40},{56,48},{64,56},{72,6... | collective-permute-start | bytes 73736 | tf_op jit(solution)/shard_map/ppermute | solution.py:32
  16.0 3.0 %scatter_custom_fusion = f32[3,8192]{0,1:T(8,128)} fusion(s32[64]{0:T(128)S(1)} %fusion.132, f32[64,3]{1,0:T(8,128)S(1)} %copy.90, f32[]{:T(128)} %constant.19.clone.1), kind=kCustom, calls=%fused_computation.1 | custom fusion | flops 192 | bytes 98308 | tf_op jit(solution)/shard_map/vmap()/scatter-add | solution.py:202
  18.9 2.9 %copy.93 = f32[1,3,4,16,128]{4,3,2,1,0:T(8,128)S(1)} copy(f32[1,3,4,16,128]{1,4,3,2,0:T(8,128)} %bitcast.451) | data formatting | bytes 196608 | tf_op jit(solution)/shard_map/reshape | solution.py:204
  24.2 3.9 %collective-permute-start.3 = (f32[1,3,1,16,128]{4,3,2,1,0:T(8,128)S(1)}, f32[1,3,1,16,128]{4,3,2,1,0:T(8,128)S(1)}, u32[]{:S(2)}, u32[]{:S(2)}) collective-permute-start(f32[1,3,1,16,128]{4,3,2,1,0:T(8,128)S(1)} %get-tuple-element.96), channel_id=1, source_target_pairs={{0,8},{8,16},{16,24},{24,32},{32,40},{40,48},{48,56},{56,64},{64,7... | collective-permute-start | bytes 73736 | tf_op jit(solution)/shard_map/ppermute | solution.py:30
  28.1 1.9 collective-permute-start.4
  30.1 4.4 %collective-permute-done.4 = f32[1,3,1,16,128]{4,3,2,1,0:T(8,128)S(1)} collective-permute-done((f32[1,3,1,16,128]{4,3,2,1,0:T(8,128)S(1)}, f32[1,3,1,16,128]{4,3,2,1,0:T(8,128)S(1)}, u32[]{:S(2)}, u32[]{:S(2)}) %collective-permute-start.4) | collective-permute-done | bytes 24608 | tf_op jit(solution)/shard_map/ppermute | solution.py:32
  36.7 2.0 collective-permute-start.5
  38.7 2.3 %collective-permute-start.6 = (f32[1,3,1,16,128]{4,3,2,1,0:T(8,128)S(1)}, f32[1,3,1,16,128]{4,3,2,1,0:T(8,128)S(1)}, u32[]{:S(2)}, u32[]{:S(2)}) collective-permute-start(f32[1,3,1,16,128]{4,3,2,1,0:T(8,128)S(1)} %get-tuple-element.93), channel_id=1, source_target_pairs={{8,0},{16,8},{24,16},{32,24},{40,32},{48,40},{56,48},{64,56},{72,6... | collective-permute-start | bytes 73736 | tf_op jit(solution)/shard_map/ppermute | solution.py:32
  41.0 6.2 %collective-permute-done.6 = f32[1,3,1,16,128]{4,3,2,1,0:T(8,128)S(1)} collective-permute-done((f32[1,3,1,16,128]{4,3,2,1,0:T(8,128)S(1)}, f32[1,3,1,16,128]{4,3,2,1,0:T(8,128)S(1)}, u32[]{:S(2)}, u32[]{:S(2)}) %collective-permute-start.6) | collective-permute-done | bytes 24608 | tf_op jit(solution)/shard_map/ppermute | solution.py:32
  49.5 1.9 collective-permute-start.7
  51.5 4.5 %collective-permute-start.9 = (f32[1,3,1,16,128]{4,3,2,1,0:T(8,128)S(1)}, f32[1,3,1,16,128]{4,3,2,1,0:T(8,128)S(1)}, u32[]{:S(2)}, u32[]{:S(2)}) collective-permute-start(f32[1,3,1,16,128]{4,3,2,1,0:T(8,128)S(1)} %get-tuple-element.92), channel_id=1, source_target_pairs={{0,8},{8,16},{16,24},{24,32},{32,40},{40,48},{48,56},{56,64},{64,7... | collective-permute-start | bytes 73736 | tf_op jit(solution)/shard_map/ppermute | solution.py:30
  56.0 1.9 collective-permute-start.10
  60.8 4.0 %all-to-all-start = ((f32[8,4,16,128]{3,2,1,0:T(8,128)}), f32[8,4,16,128]{3,2,1,0:T(8,128)S(1)}, u32[]{:S(2)}, u32[]{:S(2)}) async-start(f32[8,4,16,128]{3,2,1,0:T(8,128)} %broadcast_in_dim.19), calls=%async_computation | async-start | bytes 524288 | tf_op jit(solution)/shard_map/all_to_all | solution.py:47
  65.3 5.7 %all-to-all-done = f32[8,4,16,128]{3,2,1,0:T(8,128)S(1)} async-done(((f32[8,4,16,128]{3,2,1,0:T(8,128)}), f32[8,4,16,128]{3,2,1,0:T(8,128)S(1)}, u32[]{:S(2)}, u32[]{:S(2)}) %all-to-all-start) | async-done | bytes 262176 | tf_op jit(solution)/shard_map/all_to_all | solution.py:47
  71.6 23.5 %all-reduce.73 = (f32[]{:T(128)}, f32[]{:T(128)}) all-reduce(f32[]{:T(128)} %get-tuple-element.3, f32[]{:T(128)} %get-tuple-element.2), channel_id=1, replica_groups=mesh['slab_0'=8,'slab_1'=4,'slab_2'=2,'load'=8] {'slab_0'}, use_global_device_ids=true, to_apply=%region_4.5 | all-reduce | flops 2 | bytes 16 | tf_op jit(solution)/shard_map/psum | solution.py:56
  95.1 13.4 %all-reduce.75 = (f32[]{:T(128)}, f32[]{:T(128)}) all-reduce(f32[]{:T(128)} %get-tuple-element.8, f32[]{:T(128)} %get-tuple-element.9), channel_id=1, replica_groups=mesh['slab_0'=8,'slab_1'=4,'slab_2'=2,'load'=8] {'slab_1'}, use_global_device_ids=true, to_apply=%region_5.6 | all-reduce | flops 2 | bytes 16 | tf_op jit(solution)/shard_map/psum | solution.py:56
  108.5 9.4 %all-reduce.77 = (f32[]{:T(128)}, f32[]{:T(128)}) all-reduce(f32[]{:T(128)} %get-tuple-element.12, f32[]{:T(128)} %get-tuple-element.13), channel_id=1, replica_groups=mesh['slab_0'=8,'slab_1'=4,'slab_2'=2,'load'=8] {'slab_2'}, use_global_device_ids=true, to_apply=%region_6.7 | all-reduce | flops 2 | bytes 16 | tf_op jit(solution)/shard_map/psum | solution.py:56
  119.3 4.9 %collective-permute-start.8 = (f32[1,16,128]{2,1,0:T(8,128)S(1)}, f32[1,16,128]{2,1,0:T(8,128)S(1)}, u32[]{:S(2)}, u32[]{:S(2)}) collective-permute-start(f32[1,16,128]{2,1,0:T(8,128)S(1)} %slice.676), channel_id=1, source_target_pairs={{0,8},{8,16},{16,24},{24,32},{32,40},{40,48},{48,56},{56,64},{64,7... | collective-permute-start | bytes 24584 | tf_op jit(solution)/shard_map/ppermute | solution.py:42
  126.7 5.1 %collective-permute-start.11 = (f32[1,3,1,16,128]{4,3,2,1,0:T(8,128)S(1)}, f32[1,3,1,16,128]{4,3,2,1,0:T(8,128)S(1)}, u32[]{:S(2)}, u32[]{:S(2)}) collective-permute-start(f32[1,3,1,16,128]{4,3,2,1,0:T(8,128)S(1)} %get-tuple-element.90), channel_id=1, source_target_pairs={{0,8},{8,16},{16,24},{24,32},{32,40},{40,48},{48,56},{56,64},{64,7... | collective-permute-start | bytes 73736 | tf_op jit(solution)/shard_map/ppermute | solution.py:30
  131.8 1.9 collective-permute-start.12
  133.8 4.1 %collective-permute-done.12 = f32[1,3,1,16,128]{4,3,2,1,0:T(8,128)S(1)} collective-permute-done((f32[1,3,1,16,128]{4,3,2,1,0:T(8,128)S(1)}, f32[1,3,1,16,128]{4,3,2,1,0:T(8,128)S(1)}, u32[]{:S(2)}, u32[]{:S(2)}) %collective-permute-start.12) | collective-permute-done | bytes 24608 | tf_op jit(solution)/shard_map/ppermute | solution.py:32
  140.1 1.9 collective-permute-start.13
  142.0 2.4 %collective-permute-start.14 = (f32[1,3,1,16,128]{4,3,2,1,0:T(8,128)S(1)}, f32[1,3,1,16,128]{4,3,2,1,0:T(8,128)S(1)}, u32[]{:S(2)}, u32[]{:S(2)}) collective-permute-start(f32[1,3,1,16,128]{4,3,2,1,0:T(8,128)S(1)} %get-tuple-element.87), channel_id=1, source_target_pairs={{8,0},{16,8},{24,16},{32,24},{40,32},{48,40},{56,48},{64,56},{72,6... | collective-permute-start | bytes 73736 | tf_op jit(solution)/shard_map/ppermute | solution.py:32
  144.4 3.6 %collective-permute-done.14 = f32[1,3,1,16,128]{4,3,2,1,0:T(8,128)S(1)} collective-permute-done((f32[1,3,1,16,128]{4,3,2,1,0:T(8,128)S(1)}, f32[1,3,1,16,128]{4,3,2,1,0:T(8,128)S(1)}, u32[]{:S(2)}, u32[]{:S(2)}) %collective-permute-start.14) | collective-permute-done | bytes 24608 | tf_op jit(solution)/shard_map/ppermute | solution.py:32
  152.2 4.1 %collective-permute-done.15 = f32[1,3,1,16,128]{4,3,2,1,0:T(8,128)S(1)} collective-permute-done((f32[1,3,1,16,128]{4,3,2,1,0:T(8,128)S(1)}, f32[1,3,1,16,128]{4,3,2,1,0:T(8,128)S(1)}, u32[]{:S(2)}, u32[]{:S(2)}) %collective-permute-start.15) | collective-permute-done | bytes 24608 | tf_op jit(solution)/shard_map/ppermute | solution.py:32
  159.1 3.4 %all-to-all-start.1 = ((f32[8,4,16,128]{3,2,1,0:T(8,128)}), f32[8,4,16,128]{3,2,1,0:T(8,128)S(1)}, u32[]{:S(2)}, u32[]{:S(2)}) async-start(f32[8,4,16,128]{3,2,1,0:T(8,128)} %broadcast_in_dim.20), calls=%async_computation.1 | async-start | bytes 524288 | tf_op jit(solution)/shard_map/all_to_all | solution.py:47
  162.6 6.1 %all-to-all-done.1 = f32[8,4,16,128]{3,2,1,0:T(8,128)S(1)} async-done(((f32[8,4,16,128]{3,2,1,0:T(8,128)}), f32[8,4,16,128]{3,2,1,0:T(8,128)S(1)}, u32[]{:S(2)}, u32[]{:S(2)}) %all-to-all-start.1) | async-done | bytes 262176 | tf_op jit(solution)/shard_map/all_to_all | solution.py:47
  169.3 15.5 %all-reduce.72 = (f32[]{:T(128)}, f32[]{:T(128)}) all-reduce(f32[]{:T(128)} %get-tuple-element.5, f32[]{:T(128)} %get-tuple-element.4), channel_id=1, replica_groups=mesh['slab_0'=8,'slab_1'=4,'slab_2'=2,'load'=8] {'slab_0'}, use_global_device_ids=true, to_apply=%region_14.15 | all-reduce | flops 2 | bytes 16 | tf_op jit(solution)/shard_map/psum | solution.py:56
  184.8 20.3 %all-reduce.74 = (f32[]{:T(128)}, f32[]{:T(128)}) all-reduce(f32[]{:T(128)} %get-tuple-element.6, f32[]{:T(128)} %get-tuple-element.7), channel_id=1, replica_groups=mesh['slab_0'=8,'slab_1'=4,'slab_2'=2,'load'=8] {'slab_1'}, use_global_device_ids=true, to_apply=%region_15.16 | all-reduce | flops 2 | bytes 16 | tf_op jit(solution)/shard_map/psum | solution.py:56
  205.0 3.1 %all-reduce.76 = (f32[]{:T(128)}, f32[]{:T(128)}) all-reduce(f32[]{:T(128)} %get-tuple-element.10, f32[]{:T(128)} %get-tuple-element.11), channel_id=1, replica_groups=mesh['slab_0'=8,'slab_1'=4,'slab_2'=2,'load'=8] {'slab_2'}, use_global_device_ids=true, to_apply=%region_16.17 | all-reduce | flops 2 | bytes 16 | tf_op jit(solution)/shard_map/psum | solution.py:56
  (153 shorter events, 26.9 us)
Async XLA Ops:
  1.4 20.4 %collective-permute-start = (f32[1,16,128]{2,1,0:T(8,128)S(1)}, f32[1,16,128]{2,1,0:T(8,128)S(1)}, u32[]{:S(2)}, u32[]{:S(2)}) collective-permute-start(f32[1,16,128]{2,1,0:T(8,128)S(1)} %slice.616), channel_id=1, source_target_pairs={{0,8},{8,16},{16,24},{24,32},{32,40},{40,48},{48,56},{56,64},{64,7... | collective-permute-start | bytes 24584 | tf_op jit(solution)/shard_map/ppermute | solution.py:42
  8.7 13.2 %collective-permute-start.1 = (f32[1,3,1,16,128]{4,3,2,1,0:T(8,128)S(1)}, f32[1,3,1,16,128]{4,3,2,1,0:T(8,128)S(1)}, u32[]{:S(2)}, u32[]{:S(2)}) collective-permute-start(f32[1,3,1,16,128]{4,3,2,1,0:T(8,128)S(1)} %get-tuple-element.98), channel_id=1, source_target_pairs={{0,8},{8,16},{16,24},{24,32},{32,40},{40,48},{48,56},{56,64},{64,7... | collective-permute-start | bytes 73736 | tf_op jit(solution)/shard_map/ppermute | solution.py:30
  10.7 11.3 %collective-permute-start.2 = (f32[1,3,1,16,128]{4,3,2,1,0:T(8,128)S(1)}, f32[1,3,1,16,128]{4,3,2,1,0:T(8,128)S(1)}, u32[]{:S(2)}, u32[]{:S(2)}) collective-permute-start(f32[1,3,1,16,128]{4,3,2,1,0:T(8,128)S(1)} %get-tuple-element.97), channel_id=1, source_target_pairs={{8,0},{16,8},{24,16},{32,24},{40,32},{48,40},{56,48},{64,56},{72,6... | collective-permute-start | bytes 73736 | tf_op jit(solution)/shard_map/ppermute | solution.py:32
  15.9 5.9 %copy-start.3 = (s32[4,16,128]{2,1,0:T(8,128)S(1)}, s32[4,16,128]{2,1,0:T(8,128)}, u32[]{:S(2)}) copy-start(s32[4,16,128]{2,1,0:T(8,128)} %param.10) | copy-start | bytes 98308
  18.9 3.6 %copy-start.1 = (f32[24,24,1,1]{1,0,3,2:T(8,128)S(1)}, f32[24,24,1,1]{1,0,3,2:T(8,128)}, u32[]{:S(2)}) copy-start(f32[24,24,1,1]{1,0,3,2:T(8,128)} %constant.223) | copy-start | bytes 6916
  24.2 5.9 %collective-permute-start.3 = (f32[1,3,1,16,128]{4,3,2,1,0:T(8,128)S(1)}, f32[1,3,1,16,128]{4,3,2,1,0:T(8,128)S(1)}, u32[]{:S(2)}, u32[]{:S(2)}) collective-permute-start(f32[1,3,1,16,128]{4,3,2,1,0:T(8,128)S(1)} %get-tuple-element.96), channel_id=1, source_target_pairs={{0,8},{8,16},{16,24},{24,32},{32,40},{40,48},{48,56},{56,64},{64,7... | collective-permute-start | bytes 73736 | tf_op jit(solution)/shard_map/ppermute | solution.py:30
  28.1 6.3 %collective-permute-start.4 = (f32[1,3,1,16,128]{4,3,2,1,0:T(8,128)S(1)}, f32[1,3,1,16,128]{4,3,2,1,0:T(8,128)S(1)}, u32[]{:S(2)}, u32[]{:S(2)}) collective-permute-start(f32[1,3,1,16,128]{4,3,2,1,0:T(8,128)S(1)} %get-tuple-element.95), channel_id=1, source_target_pairs={{8,0},{16,8},{24,16},{32,24},{40,32},{48,40},{56,48},{64,56},{72,6... | collective-permute-start | bytes 73736 | tf_op jit(solution)/shard_map/ppermute | solution.py:32
  36.7 4.3 %collective-permute-start.5 = (f32[1,3,1,16,128]{4,3,2,1,0:T(8,128)S(1)}, f32[1,3,1,16,128]{4,3,2,1,0:T(8,128)S(1)}, u32[]{:S(2)}, u32[]{:S(2)}) collective-permute-start(f32[1,3,1,16,128]{4,3,2,1,0:T(8,128)S(1)} %get-tuple-element.94), channel_id=1, source_target_pairs={{0,8},{8,16},{16,24},{24,32},{32,40},{40,48},{48,56},{56,64},{64,7... | collective-permute-start | bytes 73736 | tf_op jit(solution)/shard_map/ppermute | solution.py:30
  38.7 8.6 %collective-permute-start.6 = (f32[1,3,1,16,128]{4,3,2,1,0:T(8,128)S(1)}, f32[1,3,1,16,128]{4,3,2,1,0:T(8,128)S(1)}, u32[]{:S(2)}, u32[]{:S(2)}) collective-permute-start(f32[1,3,1,16,128]{4,3,2,1,0:T(8,128)S(1)} %get-tuple-element.93), channel_id=1, source_target_pairs={{8,0},{16,8},{24,16},{32,24},{40,32},{48,40},{56,48},{64,56},{72,6... | collective-permute-start | bytes 73736 | tf_op jit(solution)/shard_map/ppermute | solution.py:32
  41.0 8.2 %copy-start.2 = (f32[1,3,4,16,128]{4,3,2,1,0:T(8,128)S(1)}, f32[1,3,4,16,128]{4,3,2,1,0:T(8,128)}, u32[]{:S(2)}) copy-start(f32[1,3,4,16,128]{4,3,2,1,0:T(8,128)} %param.11) | copy-start | bytes 294916
  49.3 21.7 %copy-start.4 = (f32[4,16,128]{2,1,0:T(8,128)S(1)}, f32[4,16,128]{2,1,0:T(8,128)}, u32[]{:S(2)}) copy-start(f32[4,16,128]{2,1,0:T(8,128)} %param.8) | copy-start | bytes 98308
  49.3 21.7 %copy-start.5 = (s32[4,16,128]{2,1,0:T(8,128)S(1)}, s32[4,16,128]{2,1,0:T(8,128)}, u32[]{:S(2)}) copy-start(s32[4,16,128]{2,1,0:T(8,128)} %param.9) | copy-start | bytes 98308
  49.5 8.4 %collective-permute-start.7 = (f32[1,3,1,16,128]{4,3,2,1,0:T(8,128)S(1)}, f32[1,3,1,16,128]{4,3,2,1,0:T(8,128)S(1)}, u32[]{:S(2)}, u32[]{:S(2)}) collective-permute-start(f32[1,3,1,16,128]{4,3,2,1,0:T(8,128)S(1)} %slice.673), channel_id=1, source_target_pairs={{8,0},{16,8},{24,16},{32,24},{40,32},{48,40},{56,48},{64,56},{72,6... | collective-permute-start | bytes 73736 | tf_op jit(solution)/shard_map/ppermute | solution.py:32
  51.5 13.3 %collective-permute-start.9 = (f32[1,3,1,16,128]{4,3,2,1,0:T(8,128)S(1)}, f32[1,3,1,16,128]{4,3,2,1,0:T(8,128)S(1)}, u32[]{:S(2)}, u32[]{:S(2)}) collective-permute-start(f32[1,3,1,16,128]{4,3,2,1,0:T(8,128)S(1)} %get-tuple-element.92), channel_id=1, source_target_pairs={{0,8},{8,16},{16,24},{24,32},{32,40},{40,48},{48,56},{56,64},{64,7... | collective-permute-start | bytes 73736 | tf_op jit(solution)/shard_map/ppermute | solution.py:30
  56.0 8.8 %collective-permute-start.10 = (f32[1,3,1,16,128]{4,3,2,1,0:T(8,128)S(1)}, f32[1,3,1,16,128]{4,3,2,1,0:T(8,128)S(1)}, u32[]{:S(2)}, u32[]{:S(2)}) collective-permute-start(f32[1,3,1,16,128]{4,3,2,1,0:T(8,128)S(1)} %get-tuple-element.91), channel_id=1, source_target_pairs={{8,0},{16,8},{24,16},{32,24},{40,32},{48,40},{56,48},{64,56},{72,6... | collective-permute-start | bytes 73736 | tf_op jit(solution)/shard_map/ppermute | solution.py:32
  60.8 10.2 %all-to-all-start = ((f32[8,4,16,128]{3,2,1,0:T(8,128)}), f32[8,4,16,128]{3,2,1,0:T(8,128)S(1)}, u32[]{:S(2)}, u32[]{:S(2)}) async-start(f32[8,4,16,128]{3,2,1,0:T(8,128)} %broadcast_in_dim.19), calls=%async_computation | async-start | bytes 524288 | tf_op jit(solution)/shard_map/all_to_all | solution.py:47
  119.3 5.5 %collective-permute-start.8 = (f32[1,16,128]{2,1,0:T(8,128)S(1)}, f32[1,16,128]{2,1,0:T(8,128)S(1)}, u32[]{:S(2)}, u32[]{:S(2)}) collective-permute-start(f32[1,16,128]{2,1,0:T(8,128)S(1)} %slice.676), channel_id=1, source_target_pairs={{0,8},{8,16},{16,24},{24,32},{32,40},{40,48},{48,56},{56,64},{64,7... | collective-permute-start | bytes 24584 | tf_op jit(solution)/shard_map/ppermute | solution.py:42
  126.7 7.0 %collective-permute-start.11 = (f32[1,3,1,16,128]{4,3,2,1,0:T(8,128)S(1)}, f32[1,3,1,16,128]{4,3,2,1,0:T(8,128)S(1)}, u32[]{:S(2)}, u32[]{:S(2)}) collective-permute-start(f32[1,3,1,16,128]{4,3,2,1,0:T(8,128)S(1)} %get-tuple-element.90), channel_id=1, source_target_pairs={{0,8},{8,16},{16,24},{24,32},{32,40},{40,48},{48,56},{56,64},{64,7... | collective-permute-start | bytes 73736 | tf_op jit(solution)/shard_map/ppermute | solution.py:30
  131.8 6.0 %collective-permute-start.12 = (f32[1,3,1,16,128]{4,3,2,1,0:T(8,128)S(1)}, f32[1,3,1,16,128]{4,3,2,1,0:T(8,128)S(1)}, u32[]{:S(2)}, u32[]{:S(2)}) collective-permute-start(f32[1,3,1,16,128]{4,3,2,1,0:T(8,128)S(1)} %get-tuple-element.89), channel_id=1, source_target_pairs={{8,0},{16,8},{24,16},{32,24},{40,32},{48,40},{56,48},{64,56},{72,6... | collective-permute-start | bytes 73736 | tf_op jit(solution)/shard_map/ppermute | solution.py:32
  140.1 4.3 %collective-permute-start.13 = (f32[1,3,1,16,128]{4,3,2,1,0:T(8,128)S(1)}, f32[1,3,1,16,128]{4,3,2,1,0:T(8,128)S(1)}, u32[]{:S(2)}, u32[]{:S(2)}) collective-permute-start(f32[1,3,1,16,128]{4,3,2,1,0:T(8,128)S(1)} %get-tuple-element.88), channel_id=1, source_target_pairs={{0,8},{8,16},{16,24},{24,32},{32,40},{40,48},{48,56},{56,64},{64,7... | collective-permute-start | bytes 73736 | tf_op jit(solution)/shard_map/ppermute | solution.py:30
  142.0 6.0 %collective-permute-start.14 = (f32[1,3,1,16,128]{4,3,2,1,0:T(8,128)S(1)}, f32[1,3,1,16,128]{4,3,2,1,0:T(8,128)S(1)}, u32[]{:S(2)}, u32[]{:S(2)}) collective-permute-start(f32[1,3,1,16,128]{4,3,2,1,0:T(8,128)S(1)} %get-tuple-element.87), channel_id=1, source_target_pairs={{8,0},{16,8},{24,16},{32,24},{40,32},{48,40},{56,48},{64,56},{72,6... | collective-permute-start | bytes 73736 | tf_op jit(solution)/shard_map/ppermute | solution.py:32
  150.2 59.8 %copy-start = (f32[1,3,4,16,128]{4,3,2,1,0:T(8,128)}, f32[1,3,4,16,128]{4,3,2,1,0:T(8,128)S(1)}, u32[]{:S(2)}) copy-start(f32[1,3,4,16,128]{4,3,2,1,0:T(8,128)S(1)} %get-tuple-element.20) | copy-start | bytes 294916
  150.3 6.0 %collective-permute-start.15 = (f32[1,3,1,16,128]{4,3,2,1,0:T(8,128)S(1)}, f32[1,3,1,16,128]{4,3,2,1,0:T(8,128)S(1)}, u32[]{:S(2)}, u32[]{:S(2)}) collective-permute-start(f32[1,3,1,16,128]{4,3,2,1,0:T(8,128)S(1)} %slice.733), channel_id=1, source_target_pairs={{8,0},{16,8},{24,16},{32,24},{40,32},{48,40},{56,48},{64,56},{72,6... | collective-permute-start | bytes 73736 | tf_op jit(solution)/shard_map/ppermute | solution.py:32
  159.1 9.5 %all-to-all-start.1 = ((f32[8,4,16,128]{3,2,1,0:T(8,128)}), f32[8,4,16,128]{3,2,1,0:T(8,128)S(1)}, u32[]{:S(2)}, u32[]{:S(2)}) async-start(f32[8,4,16,128]{3,2,1,0:T(8,128)} %broadcast_in_dim.20), calls=%async_computation.1 | async-start | bytes 524288 | tf_op jit(solution)/shard_map/all_to_all | solution.py:47
where the time goes:
time: 211 us; the launch traced here: 210 us
  blocking collectives  85.2 us (40%)
  starting transfers between devices  55.5 us (26%)
  waiting for transfers between devices  34.7 us (16%)
  matrix products  10.6 us (5%)
  local copies, waits for them, and re-layouts  9.92 us (5%)
  other arithmetic  9.78 us (5%)
  between operations  4.39 us (2%)
    psum x6, blocking collectives, by_axis(): return functools.reduce(lax.psum, axes, shard)  85.2 us
    ppermute x8, waiting for transfers between devices, with_halo(): lax.ppermute(head, axis, [((i + 1) % count, i) for i in range(ends)])  22.4 us
    ppermute x6, starting transfers between devices, with_halo(): lax.ppermute(tail, axis, [(i, (i + 1) % count) for i in range(ends)])  19.4 us
    ppermute x8, starting transfers between devices, with_halo(): lax.ppermute(head, axis, [((i + 1) % count, i) for i in range(ends)])  18.1 us
    all_to_all x2, waiting for transfers between devices, from_everyone(): return lax.all_to_all(copies, axis, split_axis=0, concat_axis=0, tiled=True)  11.8 us
    dot_general x8, matrix products, stiff_apply(): jnp.einsum('ij,cjzyx->cizyx', table, values, precision=lax.Precision.HIGH...  10.6 us
    ppermute x2, starting transfers between devices, passed_along(): lax.ppermute(value, axis, [(source, source + steps) for source in range(l...  10.5 us
    all_to_all x2, starting transfers between devices, from_everyone(): return lax.all_to_all(copies, axis, split_axis=0, concat_axis=0, tiled=True)  7.43 us
  transfers between devices with their start and end apart: 18, of which 8 were waited for; matrix products, arithmetic and copies ran while one was open for 6% of the time, Pallas kernels for 0%

commit v1 on v0

v1 whole, which is shorter than its diff:
```python
import functools
import math

import jax
import jax.numpy as jnp
import numpy as np
from jax import lax
from jax.experimental import pallas as pl
from jax.experimental.pallas import tpu as pltpu
from jax.sharding import PartitionSpec as P

SWEEPS = 3
UPDATES = 2
MESH = pl.DeviceIdType.MESH
young_floor = 0.001
density_floor = 0.001
move_limit = 0.2
sens_shift = 0.001
BELOW = 3
ABOVE = 4


def diagonal_of(matrix):
    return np.array([matrix[entry, entry] for entry in range(matrix.shape[0])])


def element_stiffness():
    poisson = 0.3
    lame_first = poisson / ((1.0 + poisson) * (1.0 - 2.0 * poisson))
    lame_second = 1.0 / (2.0 * (1.0 + poisson))
    elastic = np.zeros((6, 6))
    elastic[:3, :3] = lame_first
    for axis_pos in range(3):
        elastic[axis_pos, axis_pos] += 2.0 * lame_second
        elastic[axis_pos + 3, axis_pos + 3] = lame_second
    points = [0.5 - 0.5 / math.sqrt(3.0), 0.5 + 0.5 / math.sqrt(3.0)]
    matrix = np.zeros((24, 24))
    for point_x in points:
        for point_y in points:
            for point_z in points:
                strain = np.zeros((6, 24))
                for corner in range(8):
                    shift_x = corner % 2
                    shift_y = corner // 2 % 2
                    shift_z = corner // 4
                    value_x = point_x if shift_x else 1.0 - point_x
                    value_y = point_y if shift_y else 1.0 - point_y
                    value_z = point_z if shift_z else 1.0 - point_z
                    slope_x = 1.0 if shift_x else -1.0
                    slope_y = 1.0 if shift_y else -1.0
                    slope_z = 1.0 if shift_z else -1.0
                    grad_x = slope_x * value_y * value_z
                    grad_y = value_x * slope_y * value_z
                    grad_z = value_x * value_y * slope_z
                    column = 3 * corner
                    strain[0, column] = grad_x
                    strain[1, column + 1] = grad_y
                    strain[2, column + 2] = grad_z
                    strain[3, column] = grad_y
                    strain[3, column + 1] = grad_x
                    strain[4, column + 1] = grad_z
                    strain[4, column + 2] = grad_y
                    strain[5, column] = grad_z
                    strain[5, column + 2] = grad_x
                matrix += strain.T @ elastic @ strain / 8.0
    return matrix


def spectrum_top(matrix):
    diag_np = diagonal_of(matrix)
    scaled = matrix / np.sqrt(np.outer(diag_np, diag_np))
    vector = np.linspace(1.0, 2.0, 24)
    for repeat in range(500):
        vector = scaled @ vector
        vector = vector / np.sqrt(np.sum(vector * vector))
    return float(vector @ scaled @ vector)


def cheb_constants(matrix):
    upper_bound = 1.05 * spectrum_top(matrix)
    lower_bound = upper_bound / 12.0
    center = 0.5 * (upper_bound + lower_bound)
    half_width = 0.5 * (upper_bound - lower_bound)
    return (center, half_width, center / half_width)


def cheb_weights(count, half_width, ratio_sigma):
    weights = []
    current = 1.0 / ratio_sigma
    for iteration in range(count):
        following = 1.0 / (2.0 * ratio_sigma - current)
        weights.append((following * current, 2.0 * following / half_width))
        current = following
    return weights


def parity_stiffness(matrix):
    transform = np.zeros((24, 24))
    for mode in range(8):
        for corner in range(8):
            sign = 1.0
            for axis in range(3):
                if (mode >> axis) & 1 and not (corner >> axis) & 1:
                    sign = -sign
            for part in range(3):
                transform[3 * mode + part, 3 * corner + part] = sign
    return transform @ matrix @ transform.T / 64.0


def mode_constants(matrix):
    block = parity_stiffness(matrix)

    def entry(part_a, mode_a, part_b, mode_b):
        def index(part, mode):
            return 3 * sum(1 << axis for axis in range(3) if mode[axis] == "d") + part

        return float(block[index(part_a, mode_a), index(part_b, mode_b)])

    cross = entry(0, "dss", 1, "sds")
    return dict(
        cross=cross,
        normal=entry(0, "dss", 0, "dss") - cross,
        shear=entry(0, "sds", 1, "dss"),
        bend=entry(0, "dds", 0, "dds"),
        couple=entry(0, "dds", 2, "sdd"),
        twist=entry(0, "sdd", 1, "dsd"),
        warp=entry(0, "ddd", 0, "ddd"),
    )


def right_of(value, lane):
    return jnp.where(lane == value.shape[1] - 1, 0.0, pltpu.roll(value, value.shape[1] - 1, 1))


def left_of(value, lane):
    return jnp.where(lane == 0, 0.0, pltpu.roll(value, 1, 1))


def under_of(value, row):
    return jnp.where(row == 0, 0.0, pltpu.roll(value, 1, 0))


def plane_modes(ref, plane, lane, rows):
    found = []
    for part in range(3):
        near = ref[part, plane, 0:rows, :]
        far = ref[part, plane, 1 : rows + 1, :]
        for value in (near + far, far - near):
            other = right_of(value, lane)
            found += [value + other, other - value]
    return found


def element_modes(low, high):
    names = ("ss", "ds", "sd", "dd")
    modes = {}
    for part in range(3):
        for place, name in enumerate(names):
            low_value, high_value = low[4 * part + place], high[4 * part + place]
            if name != "ss":
                modes["xyz"[part] + name + "s"] = low_value + high_value
            modes["xyz"[part] + name + "d"] = high_value - low_value
    return modes


def stress_modes(m, young, k):
    normal, cross, shear = young * k["normal"], young * k["cross"], young * k["shear"]
    bend, couple, twist = young * k["bend"], young * k["couple"], young * k["twist"]
    warp = young * k["warp"]
    out = {}
    trace = cross * (m["xdss"] + m["ysds"] + m["zssd"])
    for name in ("xdss", "ysds", "zssd"):
        out[name] = normal * m[name] + trace
    for first, second in (("ydss", "xsds"), ("zdss", "xssd"), ("zsds", "yssd")):
        out[first] = out[second] = shear * (m[first] + m[second])
    for first, second in (("xdds", "zsdd"), ("ydds", "zdsd"), ("xdsd", "ysdd")):
        out[first] = bend * m[first] + couple * m[second]
        out[second] = couple * m[first] + bend * m[second]
    total = m["zdds"] + m["ydsd"] + m["xsdd"]
    for name in ("zdds", "ydsd", "xsdd"):
        out[name] = twist * (m[name] + total)
    for name in ("xddd", "yddd", "zddd"):
        out[name] = warp * m[name]
    return out


def energy_of(m, k):
    def squares(names):
        return sum((m[name] * m[name] for name in names[1:]), m[names[0]] * m[names[0]])

    normals = ("xdss", "ysds", "zssd")
    twists = ("zdds", "ydsd", "xsdd")
    trace = m["xdss"] + m["ysds"] + m["zssd"]
    result = k["normal"] * squares(normals) + k["cross"] * (trace * trace)
    shears = None
    for first, second in (("ydss", "xsds"), ("zdss", "xssd"), ("zsds", "yssd")):
        value = m[first] + m[second]
        shears = value * value if shears is None else shears + value * value
    result = result + k["shear"] * shears
    pairs = (("xdds", "zsdd"), ("ydds", "zdsd"), ("xdsd", "ysdd"))
    result = result + k["bend"] * squares([name for pair in pairs for name in pair])
    products = sum(
        (m[first] * m[second] for first, second in pairs[1:]), m[pairs[0][0]] * m[pairs[0][1]]
    )
    result = result + (2.0 * k["couple"]) * products
    total = m["zdds"] + m["ydsd"] + m["xsdd"]
    result = result + k["twist"] * (squares(twists) + total * total)
    return result + k["warp"] * squares(("xddd", "yddd", "zddd"))


def node_parts(out):
    lower, upper = [], []
    for part in "xyz":
        for name in ("ss", "ds", "sd", "dd"):
            odd = out[part + name + "d"]
            if name == "ss":
                lower.append(-odd)
                upper.append(odd)
            else:
                even = out[part + name + "s"]
                lower.append(even - odd)
                upper.append(even + odd)
    return lower, upper


def node_force(sums, lane, row):
    forces = []
    for part in range(3):
        both, along, across, twice = sums[4 * part : 4 * part + 4]
        even = (both - along) + left_of(both + along, lane)
        odd = (across - twice) + left_of(across + twice, lane)
        forces.append((even - odd) + under_of(even + odd, row))
    return forces


def apply_stiffness(ref, first, count, young_ref, young_first, k, lane, row, emit):
    rows = row.shape[0]
    low = plane_modes(ref, first - 1, lane, rows)
    high = plane_modes(ref, first, lane, rows)
    out = stress_modes(element_modes(low, high), young_ref[young_first - 1], k)
    pending = node_parts(out)[1]

    def step(turn, carry):
        low, pending = carry
        high = plane_modes(ref, first + 1 + turn, lane, rows)
        out = stress_modes(element_modes(low, high), young_ref[young_first + turn], k)
        lower, upper = node_parts(out)
        emit(turn, node_force([a + b for a, b in zip(lower, pending)], lane, row))
        return high, upper

    lax.fori_loop(0, count, step, (high, pending), unroll=True)


def kernel(
    k, chebyshev, stiff_diag, slabs, loads,
    density_hbm, passive_hbm, fixed_hbm, start_hbm, nodes_ref, points_ref,
    density_out, displace_out,
    fixed_buf, design_buf, passive_buf, raw_buf, masked_buf, first_dir, second_dir, final_buf,
    residual, young_buf, weight_buf, force_buf, share_design, share_active, share_energy,
    gathered_energy, gathered_q, q_buf, stage_a, stage_b, local_sem, halo_send, halo_recv,
    q_halo_send, q_halo_recv, group_send, group_recv,
):
    center, weights = chebyshev
    slab = lax.axis_index("slab")
    load = lax.axis_index("load")
    planes, rows, cols = passive_buf.shape
    own = slice(BELOW, BELOW + planes)
    lane = lax.broadcasted_iota(jnp.int32, (rows, cols), 1)
    row = lax.broadcasted_iota(jnp.int32, (rows, cols), 0)
    up = lax.rem(slab + 1, slabs)
    down = lax.rem(slab + slabs - 1, slabs)
    column = lax.div(slab, 8)
    seat = lax.rem(slab, 8)
    x_place = lax.div(load, 2)
    y_low = lax.rem(load, 2)
    me_a = seat * 2 + y_low
    me_b = column * 4 + x_place

    def member_load(step):
        other = lax.rem(load + step, loads)
        return other, (slab, other)

    def member_a(step):
        other = lax.rem(me_a + step, 16)
        return other, (column * 8 + lax.div(other, 2), x_place * 2 + lax.rem(other, 2))

    def member_b(step):
        other = lax.rem(me_b + step, 32)
        return other, (lax.div(other, 4) * 8 + seat, lax.rem(other, 4) * 2 + y_low)

    groups = ((member_load, 8), (member_a, 16), (member_b, 32))

    copies = [
        pltpu.make_async_copy(start_hbm, raw_buf.at[0, :, own], local_sem.at[0]),
        pltpu.make_async_copy(fixed_hbm, fixed_buf.at[own], local_sem.at[1]),
        pltpu.make_async_copy(density_hbm, design_buf.at[0, own], local_sem.at[2]),
        pltpu.make_async_copy(passive_hbm, passive_buf, local_sem.at[3]),
    ]
    for copy in copies:
        copy.start()

    barrier = pltpu.get_barrier_semaphore()
    for target in ((up, load), (down, load)):
        pl.semaphore_signal(barrier, inc=1, device_id=target, device_id_type=MESH)
    for member, size in groups:

        def greet(step, carry):
            pl.semaphore_signal(barrier, inc=1, device_id=member(step)[1], device_id_type=MESH)
            return carry

        lax.fori_loop(1, size, greet, 0, unroll=True)

    for copy in copies:
        copy.wait()
    for plane in range(planes):
        void = passive_buf[plane] == 1
        value = jnp.where(void, density_floor, design_buf[0, BELOW + plane])
        design_buf[0, BELOW + plane] = value
        active = 1.0 - passive_buf[plane].astype(jnp.float32)
        for part in range(loads):
            share_design[part, 2 * plane : 2 * plane + 2] = value[2 * part : 2 * part + 2]
            share_active[part, 2 * plane : 2 * plane + 2] = active[2 * part : 2 * part + 2]
    pl.semaphore_wait(barrier, 2 + sum(size - 1 for member, size in groups))

    def halo(buf, lead, upward, downward, index, send, recv):
        top = BELOW + planes
        pairs = (
            (slice(top - upward, top), slice(BELOW - upward, BELOW), up),
            (slice(BELOW, BELOW + downward), slice(top, top + downward), down),
        )
        made = []
        for place, (source, target, who) in enumerate(pairs):
            made.append(
                pltpu.make_async_remote_copy(
                    buf.at[lead + (source,)],
                    buf.at[lead + (target,)],
                    send.at[2 * index + place],
                    recv.at[2 * index + place],
                    device_id=(who, load),
                    device_id_type=MESH,
                )
            )
        for copy in made:
            copy.start()
        return made

    def send_group(group, index, source, target_of):
        member, size = groups[group]

        def go(step, carry):
            other, who = member(step)
            source_ref, target_ref = source(other), target_of
            pltpu.make_async_remote_copy(
                source_ref,
                target_ref,
                group_send.at[index],
                group_recv.at[index],
                device_id=who,
                device_id_type=MESH,
            ).start()
            return carry

        lax.fori_loop(1, size, go, 0, unroll=True)

    def await_group(sem, index, ref):
        pltpu.make_async_copy(ref, ref, sem.at[index]).wait()

    u_halos = [halo(raw_buf, (0, slice(None)), BELOW, ABOVE, 0, halo_send, halo_recv)]
    f_halo = halo(fixed_buf, (), BELOW, ABOVE, 1, halo_send, halo_recv)
    x_halo = halo(design_buf, (0,), BELOW, BELOW, 2, halo_send, halo_recv)

    edge = jnp.zeros((8, cols), jnp.float32)
    for part in range(3):
        for buf in (first_dir, second_dir, final_buf):
            for plane in range(buf.shape[1]):
                buf[part, plane, rows : rows + 8] = edge
        for plane in range(masked_buf.shape[2]):
            masked_buf[0, part, plane, rows : rows + 8] = edge
            masked_buf[1, part, plane, rows : rows + 8] = edge

    nodes = nodes_ref[...]
    points = nodes.shape[1]
    tall = 9 * rows
    place_zy = lax.broadcasted_iota(jnp.int32, (tall, points), 0) + (slab * planes - 2) * rows
    hit_zy = jnp.where(lax.div(nodes, cols) == place_zy, 1.0, 0.0)
    hit_x = lax.rem(nodes, cols) == lax.broadcasted_iota(jnp.int32, (cols, points), 0)
    for part in range(3):
        amount = jnp.where(hit_x, points_ref[0, part : part + 1, :], 0.0)
        force_buf[part] = lax.dot_general(
            hit_zy,
            amount,
            (((1,), (1,)), ((), ())),
            precision=lax.Precision.HIGHEST,
            preferred_element_type=jnp.float32,
        ).reshape(9, rows, cols)

    has_below = jnp.where(slab > 0, 1.0, 0.0)
    has_above = jnp.where(slab < slabs - 1, 1.0, 0.0)

    def young_planes(which):
        for plane in range(10):
            x = design_buf[which, plane]
            young = young_floor + (1.0 - young_floor) * x * x * x
            if plane < BELOW:
                young = young * has_below
            elif plane >= BELOW + planes:
                young = young * has_above
            young_buf[which, plane] = young

    for copies_in in (u_halos[0], f_halo, x_halo):
        for copy in copies_in:
            copy.wait_recv()

    def inverse_scale(update):
        await_group(group_recv, 4 * update + 2, stage_b.at[update, 0:31, 0:2])
        sums = jnp.sum(jnp.sum(stage_b[update, :, 0:2], axis=0), axis=1, keepdims=True)
        top, bottom = sums[0:1], sums[1:2]
        ratio = bottom / jnp.where(top > 0.0, top, 1.0)
        return jnp.where(top > 0.0, ratio, 0.0)

    for update in range(UPDATES):
        last = update == UPDATES - 1
        for plane in range(11):
            free = 1.0 - fixed_buf[plane].astype(jnp.float32)
            if plane < BELOW:
                free = free * has_below
            elif plane >= BELOW + planes:
                free = free * has_above
            for part in range(3):
                masked_buf[update, part, plane, 0:rows] = free * raw_buf[update, part, plane]
        if update:
            scale = inverse_scale(0)
            for plane in range(10):
                x = design_buf[0, plane]
                lower = jnp.maximum(density_floor, x - move_limit)
                upper = jnp.minimum(1.0, x + move_limit)
                design_buf[1, plane] = jnp.minimum(
                    jnp.maximum(q_buf[plane] * scale, lower), upper
                )
        young_planes(update)
        for node in range(9):
            free = 1.0 - fixed_buf[node + 1].astype(jnp.float32)
            if node < 2:
                free = free * has_below
            elif node >= 2 + planes:
                free = free * has_above
            around = young_buf[update, node] + young_buf[update, node + 1]
            around = around + under_of(around, row)
            around = around + left_of(around, lane)
            weight_buf[node] = free / jnp.maximum(stiff_diag * around, 1e-6)

        field = masked_buf.at[update]
        young = young_buf.at[update]

        def start_stage(turn, forces):
            weight = weight_buf[turn]
            for part in range(3):
                left = force_buf[part, turn] - forces[part]
                residual[part, turn] = left
                first_dir[part, turn, 0:rows] = (weight * left) / center

        apply_stiffness(field, 1, 9, young, 1, k, lane, row, start_stage)

        def middle_stage(turn, forces):
            weight = weight_buf[turn + 1]
            keep, push = weights[0]
            for part in range(3):
                left = residual[part, turn + 1] - forces[part]
                residual[part, turn + 1] = left
                second_dir[part, turn, 0:rows] = (
                    keep * first_dir[part, turn + 1, 0:rows] + push * weight * left
                )

        apply_stiffness(first_dir, 1, 7, young, 2, k, lane, row, middle_stage)

        def final_stage(turn, forces):
            weight = weight_buf[turn + 2]
            keep, push = weights[1]
            for part in range(3):
                left = residual[part, turn + 2] - forces[part]
                second = second_dir[part, turn + 1, 0:rows]
                final_buf[part, turn, 0:rows] = (
                    field[part, turn + BELOW, 0:rows]
                    + first_dir[part, turn + 2, 0:rows]
                    + second
                    + (keep * second + push * weight * left)
                )

        apply_stiffness(second_dir, 1, 5, young, 3, k, lane, row, final_stage)

        if not last:
            for part in range(3):
                raw_buf[1, part, own] = final_buf[part, 0:planes, 0:rows]
            u_halos.append(halo(raw_buf, (1, slice(None)), BELOW, ABOVE, 3, halo_send, halo_recv))
        else:
            writes = pltpu.make_async_copy(
                final_buf.at[:, 0:planes, 0:rows], displace_out, local_sem.at[0]
            )
            writes.start()

        low = plane_modes(final_buf, 0, lane, rows)
        for plane in range(planes):
            high = plane_modes(final_buf, plane + 1, lane, rows)
            energy = energy_of(element_modes(low, high), k)
            for part in range(loads):
                share_energy[update, part, 2 * plane : 2 * plane + 2] = energy[
                    2 * part : 2 * part + 2
                ]
            low = high
        gathered_energy[update, load] = share_energy[update, load]
        send_group(
            0, 4 * update, lambda other: share_energy.at[update, other], gathered_energy.at[update, load]
        )

        if update == 0:
            x_share = share_design[load]
        else:
            lower = jnp.maximum(density_floor, x_share - move_limit)
            upper = jnp.minimum(1.0, x_share + move_limit)
            x_share = jnp.minimum(jnp.maximum(q_share * scale, lower), upper)
        active = share_active[load]
        await_group(group_recv, 4 * update, gathered_energy.at[update, 0 : loads - 1])
        total = gathered_energy[update, 0]
        for part in range(1, loads):
            total = total + gathered_energy[update, part]
        q_share = (
            x_share
            * jnp.sqrt(3.0 * x_share * x_share * (1.0 - young_floor) * total + sens_shift)
            * active
        )
        sums = jnp.concatenate(
            [
                jnp.sum(q_share, axis=0, keepdims=True),
                jnp.sum(x_share * active, axis=0, keepdims=True),
            ],
            axis=0,
        )
        stage_a[update, me_a, 0:2] = sums
        send_group(
            1,
            4 * update + 1,
            lambda other: stage_a.at[update, me_a, 0:2],
            stage_a.at[update, me_a, 0:2],
        )
        if not last:
            gathered_q[load] = q_share
            send_group(0, 3, lambda other: gathered_q.at[load], gathered_q.at[load])
            await_group(group_recv, 3, gathered_q.at[0 : loads - 1])
            for part in range(loads):
                for plane in range(planes):
                    q_buf[BELOW + plane, 2 * part : 2 * part + 2] = gathered_q[
                        part, 2 * plane : 2 * plane + 2
                    ]
            q_halo = halo(q_buf, (), BELOW, BELOW, 0, q_halo_send, q_halo_recv)
        await_group(group_recv, 4 * update + 1, stage_a.at[update, 0:15, 0:2])
        stage_b[update, me_b, 0:2] = jnp.sum(stage_a[update, :, 0:2], axis=0)
        send_group(
            2,
            4 * update + 2,
            lambda other: stage_b.at[update, me_b, 0:2],
            stage_b.at[update, me_b, 0:2],
        )
        if not last:
            for copy in u_halos[1] + q_halo:
                copy.wait_recv()

    scale = inverse_scale(1)
    lower = jnp.maximum(density_floor, x_share - move_limit)
    upper = jnp.minimum(1.0, x_share + move_limit)
    density_out[...] = jnp.minimum(jnp.maximum(q_share * scale, lower), upper)
    writes.wait()
    for copies_out in (*u_halos, f_halo, x_halo, q_halo):
        for copy in copies_out:
            copy.wait_send()
    for update in range(UPDATES):
        await_group(group_send, 4 * update, gathered_energy.at[update, 0 : loads - 1])
        await_group(group_send, 4 * update + 1, stage_a.at[update, 0:15, 0:2])
        await_group(group_send, 4 * update + 2, stage_b.at[update, 0:31, 0:2])
    await_group(group_send, 3, gathered_q.at[0 : loads - 1])


def body(slabs, loads, density, passive, fixed, u_start, load_nodes, load_forces):
    stiff = element_stiffness()
    center, half_width, ratio_sigma = cheb_constants(stiff)
    weights = cheb_weights(SWEEPS, half_width, ratio_sigma)
    planes, rows, cols = density.shape
    wide = BELOW + planes + ABOVE
    tall = rows + 8
    f32, i32 = jnp.float32, jnp.int32
    vmem = pltpu.VMEM
    dma = pltpu.SemaphoreType.DMA
    hbm = pl.BlockSpec(memory_space=pl.ANY)
    local = pl.BlockSpec(memory_space=pltpu.VMEM)
    new_density, displacement = pl.pallas_call(
        functools.partial(
            kernel,
            mode_constants(stiff),
            (center, weights),
            float(np.mean(diagonal_of(stiff))),
            slabs,
            loads,
        ),
        out_shape=(
            jax.ShapeDtypeStruct((2 * planes, cols), f32),
            jax.ShapeDtypeStruct((3, planes, rows, cols), f32),
        ),
        in_specs=[hbm, hbm, hbm, hbm, local, local],
        out_specs=(local, hbm),
        scratch_shapes=[
            vmem((wide, rows, cols), i32),
            vmem((2, wide - 1, rows, cols), f32),
            vmem((planes, rows, cols), i32),
            vmem((2, 3, wide, rows, cols), f32),
            vmem((2, 3, wide, tall, cols), f32),
            vmem((3, wide - 2, tall, cols), f32),
            vmem((3, wide - 4, tall, cols), f32),
            vmem((3, wide - 6, tall, cols), f32),
            vmem((3, wide - 2, rows, cols), f32),
            vmem((2, wide - 1, rows, cols), f32),
            vmem((wide - 2, rows, cols), f32),
            vmem((3, wide - 2, rows, cols), f32),
            vmem((loads, 8, cols), f32),
            vmem((loads, 8, cols), f32),
            vmem((2, loads, 8, cols), f32),
            vmem((2, loads, 8, cols), f32),
            vmem((loads, 8, cols), f32),
            vmem((wide - 1, rows, cols), f32),
            vmem((2, 16, 8, cols), f32),
            vmem((2, 32, 8, cols), f32),
            dma((4,)),
            dma((8,)),
            dma((8,)),
            dma((2,)),
            dma((2,)),
            dma((8,)),
            dma((8,)),
        ],
        compiler_params=pltpu.CompilerParams(collective_id=0, has_side_effects=True),
        name="updates",
    )(density, passive, fixed, u_start[0], load_nodes, load_forces)
    return new_density.reshape(planes, 2, cols), displacement[None]


def solution(mesh):
    placed = (
        P("slab", None, None),
        P("slab", None, None),
        P("slab", None, None),
        P("load", None, "slab", None, None),
        P("load", None),
        P("load", None, None),
    )
    return jax.shard_map(
        functools.partial(body, mesh.shape["slab"], mesh.shape["load"]),
        mesh=mesh,
        in_specs=placed,
        out_specs=(P("slab", "load", None), P("load", None, "slab", None, None)),
        check_vma=False,
    )
```

time: 211 us -> 61.3 us (0.29)
  blocking collectives: 85.2 us -> 0 us
  Pallas kernels: 0 us -> 56.3 us
  starting transfers between devices: 55.5 us -> 0 us
  waiting for transfers between devices: 34.7 us -> 0 us
  matrix products: 10.6 us -> 0 us
  other arithmetic: 9.78 us -> 0 us
  local copies, waits for them, and re-layouts: 9.92 us -> 4.06 us
  between operations: 4.39 us -> 0.66 us
    psum x6 -> x0, blocking collectives: 85.2 us -> none  [by_axis(): return functools.reduce(lax.psum, axes, shard)]
    pallas_call x0 -> x1, Pallas kernels: none -> 56.3 us  [body(): pl.pallas_call(functools.partial(kernel, mode_constants(stiff), (center,...]
    ppermute x16 -> x0, starting transfers between devices: 48.1 us -> none  [the longest x6 19.4 us: with_halo(): lax.ppermute(tail, axis, [(i, (i + 1) % count) for i in range(ends)])]
    ppermute x16 -> x0, waiting for transfers between devices: 22.9 us -> none  [the longest x8 22.4 us: with_halo(): lax.ppermute(head, axis, [((i + 1) % count, i) for i in range(ends)])]
    all_to_all x2 -> x0, waiting for transfers between devices: 11.8 us -> none  [from_everyone(): return lax.all_to_all(copies, axis, split_axis=0, concat_axis=0, tiled=True)]
    dot_general x8 -> x0, matrix products: 10.6 us -> none  [stiff_apply(): jnp.einsum('ij,cjzyx->cizyx', table, values, precision=lax.Precision.HIGH...]
    all_to_all x2 -> x0, starting transfers between devices: 7.43 us -> none  [from_everyone(): return lax.all_to_all(copies, axis, split_axis=0, concat_axis=0, tiled=True)]
    scatter-add x2 -> x0, other arithmetic: 2.98 us -> none  [place(): jnp.zeros((3, count), jnp.float32).at[:, local].add(values, mode='drop')]
  transfers between devices with their start and end apart: 18 -> 0, of which waited for: 8 -> 0; matrix products, arithmetic and copies ran while one was open for 6% -> 0% of each run, Pallas kernels for 0% -> 0%
where the time goes in v1:
time: 61.3 us; the launch traced here: 61 us
  Pallas kernels  56.3 us (92%)
  local copies, waits for them, and re-layouts  4.06 us (7%)
  between operations  0.66 us (1%)
    pallas_call x1, Pallas kernels, body(): pl.pallas_call(functools.partial(kernel, mode_constants(stiff), (center,...  56.3 us
    unnamed x7, local copies, waits for them, and re-layouts  4.06 us

profile of v1, /device:TPU:1, one launch (start us, length us, event | category | flops | bytes accessed | tf_op | source)
XLA Modules:
  0.0 61.0 jit_solution(11601393381219890390)
XLA Ops:
  0.6 0.0 copy-start.1
  0.6 0.7 %copy-done.1 = f32[1,3,64]{2,0,1:T(1,128)S(1)} copy-done((f32[1,3,64]{2,0,1:T(1,128)S(1)}, f32[1,3,64]{2,0,1:T(1,128)}, u32[]{:S(2)}) %copy-start.1) | copy-done | bytes 792
  1.3 0.6 copy.8.points_ref
  1.9 56.3 %updates.1 = (f32[8,128]{1,0:T(8,128)}, f32[3,4,16,128]{3,2,1,0:T(8,128)}) custom-call(f32[4,16,128]{2,1,0:T(8,128)} %density_hbm.1, s32[4,16,128]{2,1,0:T(8,128)} %passive_hbm.1, s32[4,16,128]{2,1,0:T(8,128)} %fixed_hbm.1, f32[3,4,16,128]{3,2,1,0:T(8,128)} %bitcast.3, s32[1,64]{1,0:T(1,128)} %nodes_ref.1, f32[1,3,64]{2,1,0:T(4,128)} %copy.8.points_ref), custom_call_target="tpu_custom_call" | custom-call | tf_op jit(solution)/shard_map/updates/pallas_call | solution.py:594
  58.2 0.0 copy-start
  58.2 0.7 %copy-done = f32[8,128]{1,0:T(8,128)S(1)} copy-done((f32[8,128]{1,0:T(8,128)S(1)}, f32[8,128]{1,0:T(8,128)}, u32[]{:S(2)}) %copy-start) | copy-done | bytes 4120
  58.9 0.6 copy.11
  59.5 1.5 %copy.12 = f32[1,3,4,16,128]{4,3,2,1,0:T(8,128)} copy(f32[1,3,4,16,128]{4,3,2,1,0:T(8,128)} %bitcast.4) | data formatting | bytes 196608
Async XLA Ops:
  0.6 0.7 %copy-start.1 = (f32[1,3,64]{2,0,1:T(1,128)S(1)}, f32[1,3,64]{2,0,1:T(1,128)}, u32[]{:S(2)}) copy-start(f32[1,3,64]{2,0,1:T(1,128)} %param.11) | copy-start | bytes 2308
  58.2 0.7 %copy-start = (f32[8,128]{1,0:T(8,128)S(1)}, f32[8,128]{1,0:T(8,128)}, u32[]{:S(2)}) copy-start(f32[8,128]{1,0:T(8,128)} %get-tuple-element.4) | copy-start | bytes 12292

commit v2 on v1

--- a/solution.py
+++ b/solution.py
@@ -140,11 +140,12 @@
     return jnp.where(row == 0, 0.0, pltpu.roll(value, 1, 0))
 
 
-def plane_modes(ref, plane, lane, rows):
+def plane_modes(ref, plane, start, lane):
+    rows = lane.shape[0]
     found = []
     for part in range(3):
-        near = ref[part, plane, 0:rows, :]
-        far = ref[part, plane, 1 : rows + 1, :]
+        near = ref[part, plane, start : start + rows, :]
+        far = ref[part, plane, start + 1 : start + 1 + rows, :]
         for value in (near + far, far - near):
             other = right_of(value, lane)
             found += [value + other, other - value]
@@ -223,40 +224,53 @@
     return lower, upper
 
 
-def node_force(sums, lane, row):
-    forces = []
+def node_rows(sums, lane):
+    rows = []
     for part in range(3):
         both, along, across, twice = sums[4 * part : 4 * part + 4]
         even = (both - along) + left_of(both + along, lane)
         odd = (across - twice) + left_of(across + twice, lane)
-        forces.append((even - odd) + under_of(even + odd, row))
-    return forces
-
-
-def apply_stiffness(ref, first, count, young_ref, young_first, k, lane, row, emit):
-    rows = row.shape[0]
-    low = plane_modes(ref, first - 1, lane, rows)
-    high = plane_modes(ref, first, lane, rows)
-    out = stress_modes(element_modes(low, high), young_ref[young_first - 1], k)
-    pending = node_parts(out)[1]
-
-    def step(turn, carry):
-        low, pending = carry
-        high = plane_modes(ref, first + 1 + turn, lane, rows)
-        out = stress_modes(element_modes(low, high), young_ref[young_first + turn], k)
-        lower, upper = node_parts(out)
-        emit(turn, node_force([a + b for a, b in zip(lower, pending)], lane, row))
-        return high, upper
-
-    lax.fori_loop(0, count, step, (high, pending), unroll=True)
+        rows.append((even - odd, even + odd))
+    return rows
+
+
+def apply_stiffness(ref, first, count, young_ref, young_first, k, lane, row, seam, emit):
+    half = lane.shape[0]
+    for part_of_plane in range(2):
+        start = part_of_plane * half
+        rows = slice(start, start + half)
+        low = plane_modes(ref, first - 1, start, lane)
+        high = plane_modes(ref, first, start, lane)
+        out = stress_modes(element_modes(low, high), young_ref[young_first - 1, rows], k)
+        pending = node_parts(out)[1]
+
+        def step(turn, carry):
+            low, pending = carry
+            high = plane_modes(ref, first + 1 + turn, start, lane)
+            out = stress_modes(element_modes(low, high), young_ref[young_first + turn, rows], k)
+            lower, upper = node_parts(out)
+            forces = []
+            pairs = node_rows([a + b for a, b in zip(lower, pending)], lane)
+            for part, (near, far) in enumerate(pairs):
+                turned = pltpu.roll(far, 1, 0)
+                if start == 0:
+                    seam[part, turn] = turned
+                    above = 0.0
+                else:
+                    above = seam[part, turn]
+                forces.append(near + jnp.where(row == 0, above, turned))
+            emit(turn, rows, forces)
+            return high, upper
+
+        lax.fori_loop(0, count, step, (high, pending), unroll=True)
 
 
 def kernel(
     k, chebyshev, stiff_diag, slabs, loads,
-    density_hbm, passive_hbm, fixed_hbm, start_hbm, nodes_ref, points_ref,
+    density_hbm, passive_hbm, fixed_hbm, start_hbm, nodes_hbm, points_hbm,
     density_out, displace_out,
-    fixed_buf, design_buf, passive_buf, raw_buf, masked_buf, first_dir, second_dir, final_buf,
-    residual, young_buf, weight_buf, force_buf, share_design, share_active, share_energy,
+    nodes_ref, points_ref, fixed_buf, design_buf, passive_buf, raw_buf, masked_buf, first_dir, second_dir, final_buf,
+    residual, seam, young_buf, weight_buf, force_buf, share_design, share_active, share_energy,
     gathered_energy, gathered_q, q_buf, stage_a, stage_b, local_sem, halo_send, halo_recv,
     q_halo_send, q_halo_recv, group_send, group_recv,
 ):
@@ -267,34 +281,54 @@
     own = slice(BELOW, BELOW + planes)
     lane = lax.broadcasted_iota(jnp.int32, (rows, cols), 1)
     row = lax.broadcasted_iota(jnp.int32, (rows, cols), 0)
+    half_lane = lax.broadcasted_iota(jnp.int32, (rows // 2, cols), 1)
+    half_row = lax.broadcasted_iota(jnp.int32, (rows // 2, cols), 0)
     up = lax.rem(slab + 1, slabs)
     down = lax.rem(slab + slabs - 1, slabs)
     column = lax.div(slab, 8)
     seat = lax.rem(slab, 8)
     x_place = lax.div(load, 2)
     y_low = lax.rem(load, 2)
-    me_a = seat * 2 + y_low
+    y_place = lax.div(seat, 2) * 2 + y_low
+    core = lax.rem(seat, 2)
+    me_a = y_place * 2 + core
     me_b = column * 4 + x_place
-
-    def member_load(step):
-        other = lax.rem(load + step, loads)
-        return other, (slab, other)
-
-    def member_a(step):
-        other = lax.rem(me_a + step, 16)
-        return other, (column * 8 + lax.div(other, 2), x_place * 2 + lax.rem(other, 2))
-
-    def member_b(step):
-        other = lax.rem(me_b + step, 32)
-        return other, (lax.div(other, 4) * 8 + seat, lax.rem(other, 4) * 2 + y_low)
-
-    groups = ((member_load, 8), (member_a, 16), (member_b, 32))
+    slab_at = [lax.rem(column + step, 8) * 8 + seat for step in range(8)]
+    load_at = [lax.rem(x_place + step, 4) * 2 for step in range(4)]
+    y_at = [lax.rem(y_place + step, 8) for step in range(8)]
+    y_slab = [column * 8 + lax.div(y, 2) * 2 for y in y_at]
+    y_load = [load - y_low + lax.rem(y, 2) for y in y_at]
+    cores = (core, 1 - core)
+    lows = (y_low, 1 - y_low)
+
+    def near(step, size):
+        return min(step, size - step)
+
+    def by_distance(pairs, size, other):
+        order = sorted(pairs, key=lambda p: -(near(p[0], size) + near(p[1], other)))
+        return [p for p in order if p != (0, 0)]
+
+    over_load = [
+        (load_at[step] + lows[low], (slab, load_at[step] + lows[low]))
+        for step, low in by_distance([(i, j) for i in range(4) for j in range(2)], 4, 2)
+    ]
+    over_a = [
+        (None, (y_slab[step] + cores[flip], y_load[step]))
+        for step, flip in by_distance([(i, j) for i in range(8) for j in range(2)], 8, 2)
+    ]
+    over_b = [
+        (None, (slab_at[up_by], load_at[step] + y_low))
+        for up_by, step in by_distance([(i, j) for i in range(8) for j in range(4)], 8, 4)
+    ]
+    groups = (over_load, over_a, over_b)
 
     copies = [
         pltpu.make_async_copy(start_hbm, raw_buf.at[0, :, own], local_sem.at[0]),
         pltpu.make_async_copy(fixed_hbm, fixed_buf.at[own], local_sem.at[1]),
         pltpu.make_async_copy(density_hbm, design_buf.at[0, own], local_sem.at[2]),
         pltpu.make_async_copy(passive_hbm, passive_buf, local_sem.at[3]),
+        pltpu.make_async_copy(nodes_hbm, nodes_ref, local_sem.at[4]),
+        pltpu.make_async_copy(points_hbm, points_ref, local_sem.at[5]),
     ]
     for copy in copies:
         copy.start()
@@ -302,13 +336,9 @@
     barrier = pltpu.get_barrier_semaphore()
     for target in ((up, load), (down, load)):
         pl.semaphore_signal(barrier, inc=1, device_id=target, device_id_type=MESH)
-    for member, size in groups:
-
-        def greet(step, carry):
-            pl.semaphore_signal(barrier, inc=1, device_id=member(step)[1], device_id_type=MESH)
-            return carry
-
-        lax.fori_loop(1, size, greet, 0, unroll=True)
+    for group in groups:
+        for _, who in group:
+            pl.semaphore_signal(barrier, inc=1, device_id=who, device_id_type=MESH)
 
     for copy in copies:
         copy.wait()
@@ -320,7 +350,7 @@
         for part in range(loads):
             share_design[part, 2 * plane : 2 * plane + 2] = value[2 * part : 2 * part + 2]
             share_active[part, 2 * plane : 2 * plane + 2] = active[2 * part : 2 * part + 2]
-    pl.semaphore_wait(barrier, 2 + sum(size - 1 for member, size in groups))
+    pl.semaphore_wait(barrier, 2 + sum(len(group) for group in groups))
 
     def halo(buf, lead, upward, downward, index, send, recv):
         top = BELOW + planes
@@ -344,30 +374,23 @@
             copy.start()
         return made
 
-    def send_group(group, index, source, target_of):
-        member, size = groups[group]
-
-        def go(step, carry):
-            other, who = member(step)
-            source_ref, target_ref = source(other), target_of
+    def send_group(group, index, source, target):
+        for other, who in groups[group]:
             pltpu.make_async_remote_copy(
-                source_ref,
-                target_ref,
+                source(other),
+                target,
                 group_send.at[index],
                 group_recv.at[index],
                 device_id=who,
                 device_id_type=MESH,
             ).start()
-            return carry
-
-        lax.fori_loop(1, size, go, 0, unroll=True)
 
     def await_group(sem, index, ref):
         pltpu.make_async_copy(ref, ref, sem.at[index]).wait()
 
+    x_halo = halo(design_buf, (0,), BELOW, BELOW, 2, halo_send, halo_recv)
+    f_halo = halo(fixed_buf, (), BELOW, ABOVE, 1, halo_send, halo_recv)
     u_halos = [halo(raw_buf, (0, slice(None)), BELOW, ABOVE, 0, halo_send, halo_recv)]
-    f_halo = halo(fixed_buf, (), BELOW, ABOVE, 1, halo_send, halo_recv)
-    x_halo = halo(design_buf, (0,), BELOW, BELOW, 2, halo_send, halo_recv)
 
     edge = jnp.zeros((8, cols), jnp.float32)
     for part in range(3):
@@ -385,7 +408,7 @@
     hit_zy = jnp.where(lax.div(nodes, cols) == place_zy, 1.0, 0.0)
     hit_x = lax.rem(nodes, cols) == lax.broadcasted_iota(jnp.int32, (cols, points), 0)
     for part in range(3):
-        amount = jnp.where(hit_x, points_ref[0, part : part + 1, :], 0.0)
+        amount = jnp.where(hit_x, points_ref[part], 0.0)
         force_buf[part] = lax.dot_general(
             hit_zy,
             amount,
@@ -407,9 +430,24 @@
                 young = young * has_above
             young_buf[which, plane] = young
 
-    for copies_in in (u_halos[0], f_halo, x_halo):
-        for copy in copies_in:
-            copy.wait_recv()
+    def weights_of(update):
+        for node in range(9):
+            free = 1.0 - fixed_buf[node + 1].astype(jnp.float32)
+            if node < 2:
+                free = free * has_below
+            elif node >= 2 + planes:
+                free = free * has_above
+            around = young_buf[update, node] + young_buf[update, node + 1]
+            around = around + under_of(around, row)
+            around = around + left_of(around, lane)
+            weight_buf[node] = free / jnp.maximum(stiff_diag * around, 1e-6)
+
+    for copy in x_halo + f_halo:
+        copy.wait_recv()
+    young_planes(0)
+    weights_of(0)
+    for copy in u_halos[0]:
+        copy.wait_recv()
 
     def inverse_scale(update):
         await_group(group_recv, 4 * update + 2, stage_b.at[update, 0:31, 0:2])
@@ -437,76 +475,70 @@
                 design_buf[1, plane] = jnp.minimum(
                     jnp.maximum(q_buf[plane] * scale, lower), upper
                 )
-        young_planes(update)
-        for node in range(9):
-            free = 1.0 - fixed_buf[node + 1].astype(jnp.float32)
-            if node < 2:
-                free = free * has_below
-            elif node >= 2 + planes:
-                free = free * has_above
-            around = young_buf[update, node] + young_buf[update, node + 1]
-            around = around + under_of(around, row)
-            around = around + left_of(around, lane)
-            weight_buf[node] = free / jnp.maximum(stiff_diag * around, 1e-6)
+            young_planes(1)
+            weights_of(1)
 
         field = masked_buf.at[update]
         young = young_buf.at[update]
 
-        def start_stage(turn, forces):
-            weight = weight_buf[turn]
+        def start_stage(turn, part_rows, forces):
+            weight = weight_buf[turn, part_rows]
             for part in range(3):
-                left = force_buf[part, turn] - forces[part]
-                residual[part, turn] = left
-                first_dir[part, turn, 0:rows] = (weight * left) / center
-
-        apply_stiffness(field, 1, 9, young, 1, k, lane, row, start_stage)
-
-        def middle_stage(turn, forces):
-            weight = weight_buf[turn + 1]
+                left = force_buf[part, turn, part_rows] - forces[part]
+                residual[part, turn, part_rows] = left
+                first_dir[part, turn, part_rows] = (weight * (1.0 / center)) * left
+
+        apply_stiffness(
+            field, 1, 9, young, 1, k, half_lane, half_row, seam, start_stage
+        )
+
+        def middle_stage(turn, part_rows, forces):
             keep, push = weights[0]
+            weight = push * weight_buf[turn + 1, part_rows]
             for part in range(3):
-                left = residual[part, turn + 1] - forces[part]
-                residual[part, turn + 1] = left
-                second_dir[part, turn, 0:rows] = (
-                    keep * first_dir[part, turn + 1, 0:rows] + push * weight * left
+                left = residual[part, turn + 1, part_rows] - forces[part]
+                residual[part, turn + 1, part_rows] = left
+                second_dir[part, turn, part_rows] = (
+                    keep * first_dir[part, turn + 1, part_rows] + weight * left
                 )
 
-        apply_stiffness(first_dir, 1, 7, young, 2, k, lane, row, middle_stage)
-
-        def final_stage(turn, forces):
-            weight = weight_buf[turn + 2]
+        apply_stiffness(
+            first_dir, 1, 7, young, 2, k, half_lane, half_row, seam, middle_stage
+        )
+
+        def final_stage(turn, part_rows, forces):
             keep, push = weights[1]
+            weight = push * weight_buf[turn + 2, part_rows]
             for part in range(3):
-                left = residual[part, turn + 2] - forces[part]
-                second = second_dir[part, turn + 1, 0:rows]
-                final_buf[part, turn, 0:rows] = (
-                    field[part, turn + BELOW, 0:rows]
-                    + first_dir[part, turn + 2, 0:rows]
-                    + second
-                    + (keep * second + push * weight * left)
+                left = residual[part, turn + 2, part_rows] - forces[part]
+                final_buf[part, turn, part_rows] = (
+                    field[part, turn + BELOW, part_rows]
+                    + first_dir[part, turn + 2, part_rows]
+                    + (1.0 + keep) * second_dir[part, turn + 1, part_rows]
+                    + weight * left
                 )
 
-        apply_stiffness(second_dir, 1, 5, young, 3, k, lane, row, final_stage)
+        apply_stiffness(
+            second_dir, 1, 5, young, 3, k, half_lane, half_row, seam, final_stage
+        )
 
         if not last:
             for part in range(3):
                 raw_buf[1, part, own] = final_buf[part, 0:planes, 0:rows]
             u_halos.append(halo(raw_buf, (1, slice(None)), BELOW, ABOVE, 3, halo_send, halo_recv))
         else:
-            writes = pltpu.make_async_copy(
-                final_buf.at[:, 0:planes, 0:rows], displace_out, local_sem.at[0]
-            )
-            writes.start()
-
-        low = plane_modes(final_buf, 0, lane, rows)
-        for plane in range(planes):
-            high = plane_modes(final_buf, plane + 1, lane, rows)
-            energy = energy_of(element_modes(low, high), k)
-            for part in range(loads):
-                share_energy[update, part, 2 * plane : 2 * plane + 2] = energy[
-                    2 * part : 2 * part + 2
-                ]
-            low = high
+            displace_out[...] = final_buf[:, 0:planes, 0:rows]
+
+        for start in (0, rows // 2):
+            low = plane_modes(final_buf, 0, start, half_lane)
+            for plane in range(planes):
+                high = plane_modes(final_buf, plane + 1, start, half_lane)
+                energy = energy_of(element_modes(low, high), k)
+                for pair in range(rows // 4):
+                    share_energy[update, start // 2 + pair, 2 * plane : 2 * plane + 2] = energy[
+                        2 * pair : 2 * pair + 2
+                    ]
+                low = high
         gathered_energy[update, load] = share_energy[update, load]
         send_group(
             0, 4 * update, lambda other: share_energy.at[update, other], gathered_energy.at[update, load]
@@ -545,6 +577,15 @@
         if not last:
             gathered_q[load] = q_share
             send_group(0, 3, lambda other: gathered_q.at[load], gathered_q.at[load])
+        await_group(group_recv, 4 * update + 1, stage_a.at[update, 0:15, 0:2])
+        stage_b[update, me_b, 0:2] = jnp.sum(stage_a[update, :, 0:2], axis=0)
+        send_group(
+            2,
+            4 * update + 2,
+            lambda other: stage_b.at[update, me_b, 0:2],
+            stage_b.at[update, me_b, 0:2],
+        )
+        if not last:
             await_group(group_recv, 3, gathered_q.at[0 : loads - 1])
             for part in range(loads):
                 for plane in range(planes):
@@ -552,15 +593,6 @@
                         part, 2 * plane : 2 * plane + 2
                     ]
             q_halo = halo(q_buf, (), BELOW, BELOW, 0, q_halo_send, q_halo_recv)
-        await_group(group_recv, 4 * update + 1, stage_a.at[update, 0:15, 0:2])
-        stage_b[update, me_b, 0:2] = jnp.sum(stage_a[update, :, 0:2], axis=0)
-        send_group(
-            2,
-            4 * update + 2,
-            lambda other: stage_b.at[update, me_b, 0:2],
-            stage_b.at[update, me_b, 0:2],
-        )
-        if not last:
             for copy in u_halos[1] + q_halo:
                 copy.wait_recv()
 
@@ -568,7 +600,6 @@
     lower = jnp.maximum(density_floor, x_share - move_limit)
     upper = jnp.minimum(1.0, x_share + move_limit)
     density_out[...] = jnp.minimum(jnp.maximum(q_share * scale, lower), upper)
-    writes.wait()
     for copies_out in (*u_halos, f_halo, x_halo, q_halo):
         for copy in copies_out:
             copy.wait_send()
@@ -577,6 +608,40 @@
         await_group(group_send, 4 * update + 1, stage_a.at[update, 0:15, 0:2])
         await_group(group_send, 4 * update + 2, stage_b.at[update, 0:31, 0:2])
     await_group(group_send, 3, gathered_q.at[0 : loads - 1])
+
+
+def deliver(share, displacement):
+    parts, planes, rows, cols = displacement.shape
+
+    def kernel(share_ref, source_ref, density_out, displace_out, split, sems):
+        first = pltpu.make_async_copy(source_ref, displace_out.at[0], sems.at[0])
+        first.start()
+        for plane in range(planes):
+            split[plane] = share_ref[2 * plane : 2 * plane + 2]
+        second = pltpu.make_async_copy(split, density_out, sems.at[1])
+        second.start()
+        second.wait()
+        first.wait()
+
+    hbm = pl.BlockSpec(memory_space=pl.ANY)
+    local = pl.BlockSpec(memory_space=pltpu.VMEM)
+    return pl.pallas_call(
+        kernel,
+        out_shape=(
+            jax.ShapeDtypeStruct((planes, 2, cols), jnp.float32),
+            jax.ShapeDtypeStruct((1, parts, planes, rows, cols), jnp.float32),
+        ),
+        in_specs=[local, local],
+        out_specs=(hbm, hbm),
+        scratch_shapes=[
+            pltpu.VMEM((planes, 2, cols), jnp.float32),
+            pltpu.SemaphoreType.DMA((2,)),
+        ],
+        name="deliver",
+    )(
+        pltpu.with_memory_space_constraint(share, pltpu.VMEM),
+        pltpu.with_memory_space_constraint(displacement, pltpu.VMEM),
+    )
 
 
 def body(slabs, loads, density, passive, fixed, u_start, load_nodes, load_forces):
@@ -601,12 +666,14 @@
             loads,
         ),
         out_shape=(
-            jax.ShapeDtypeStruct((2 * planes, cols), f32),
-            jax.ShapeDtypeStruct((3, planes, rows, cols), f32),
+            pltpu.VMEM((2 * planes, cols), f32),
+            pltpu.VMEM((3, planes, rows, cols), f32),
         ),
-        in_specs=[hbm, hbm, hbm, hbm, local, local],
-        out_specs=(local, hbm),
+        in_specs=[hbm] * 6,
+        out_specs=(local, local),
         scratch_shapes=[
+            vmem(load_nodes.shape, i32),
+            vmem((3, 1, load_nodes.shape[1]), f32),
             vmem((wide, rows, cols), i32),
             vmem((2, wide - 1, rows, cols), f32),
             vmem((planes, rows, cols), i32),
@@ -616,6 +683,7 @@
             vmem((3, wide - 4, tall, cols), f32),
             vmem((3, wide - 6, tall, cols), f32),
             vmem((3, wide - 2, rows, cols), f32),
+            vmem((3, wide - 2, rows // 2, cols), f32),
             vmem((2, wide - 1, rows, cols), f32),
             vmem((wide - 2, rows, cols), f32),
             vmem((3, wide - 2, rows, cols), f32),
@@ -627,7 +695,7 @@
             vmem((wide - 1, rows, cols), f32),
             vmem((2, 16, 8, cols), f32),
             vmem((2, 32, 8, cols), f32),
-            dma((4,)),
+            dma((6,)),
             dma((8,)),
             dma((8,)),
             dma((2,)),
@@ -637,8 +705,8 @@
         ],
         compiler_params=pltpu.CompilerParams(collective_id=0, has_side_effects=True),
         name="updates",
-    )(density, passive, fixed, u_start[0], load_nodes, load_forces)
-    return new_density.reshape(planes, 2, cols), displacement[None]
+    )(density, passive, fixed, u_start[0], load_nodes, load_forces.transpose(1, 0, 2))
+    return deliver(new_density, displacement)
 
 
 def solution(mesh):

time: 61.3 us -> 57.3 us (0.935)
  local copies, waits for them, and re-layouts: 4.06 us -> 0 us
    unnamed x7 -> x0, local copies, waits for them, and re-layouts: 4.06 us -> none
    pallas_call x0 -> x1, Pallas kernels: none -> 0.66 us  [deliver(): pl.pallas_call(kernel, out_shape=(jax.ShapeDtypeStruct((planes, 2, cols),...]
where the time goes in v2:
time: 57.3 us; the launch traced here: 57.1 us
  Pallas kernels  56.5 us (99%)
  between operations  0.64 us (1%)
    pallas_call x1, Pallas kernels, body(): pl.pallas_call(functools.partial(kernel, mode_constants(stiff), (center,...  55.8 us

profile of v2, /device:TPU:1, one launch (start us, length us, event | category | flops | bytes accessed | tf_op | source)
XLA Modules:
  0.0 57.1 jit_solution(14539680241352610379)
XLA Ops:
  0.6 55.8 %updates.1 = (f32[8,128]{1,0:T(8,128)S(1)}, f32[3,4,16,128]{3,2,1,0:T(8,128)S(1)}) custom-call(f32[4,16,128]{2,1,0:T(8,128)} %density_hbm.1, s32[4,16,128]{2,1,0:T(8,128)} %passive_hbm.1, s32[4,16,128]{2,1,0:T(8,128)} %fixed_hbm.1, f32[3,4,16,128]{3,2,1,0:T(8,128)} %bitcast.2, s32[1,64]{1,0:T(1,128)} %nodes_hbm.1, f32[3,1,64]{2,1,0:T(1,128)} %bitcast.3), custom_call_target="tpu_custom_call" | custom-call | tf_op jit(solution)/shard_map/updates/pallas_call | solution.py:659
  56.5 0.7 %deliver.1 = (f32[4,2,128]{2,1,0:T(2,128)}, f32[1,3,4,16,128]{4,3,2,1,0:T(8,128)}) custom-call(f32[8,128]{1,0:T(8,128)S(1)} %get-tuple-element.4.share_ref, f32[3,4,16,128]{3,2,1,0:T(8,128)S(1)} %get-tuple-element.5.source_ref), custom_call_target="tpu_custom_call" | custom-call | tf_op jit(solution)/shard_map/deliver/pallas_call | solution.py:628
